TPU v7x, 32 devices: a whole 2x2x4 slice. The times are simulated.
32 devices in a mesh: grp: 2 (over y), slab: 4 (over z), orb: 2 (over x), rep: 2 (over core).
Axes of the slice: x: 2, y: 2, z: 4, core: 2. Of those that a mesh axis runs over, the one named last changes fastest.
Arguments:
- orbitals: bfloat16 [16, 32, 1024], P(('grp', 'slab', 'orb')), parts along dimension 0, may hold values from -6 to 6
- corners: int32 [16, 3], P('grp'), parts along dimension 0, may hold values from 0 to 191, as said below
- partners: int32 [16, 24], P(('grp', 'slab', 'orb')), parts along dimension 0, may hold values from -1 to 7, as said below
- kernel: float32 [32, 1024], replicated, may hold values from 0.05 to 5
Outputs:
- exchange_boxes: float32 [16, 32, 1024], P(('grp', 'slab', 'orb')), parts along dimension 0
- exchange_energy: float32 [2], P('grp'), parts along dimension 0
There are 2 independent parts, one for each index of `grp`. A program takes and returns all parts, laid end to end along the dimension named above; an argument that names none is the same for every part. Nothing has to cross between parts.
Inputs may be any that keep to these rules, and one draw needn't show every extreme that they name: corners[i, 2] lies in the slab of orbital i: from 12 * (i // (1 * 2)) to 12 more less one; corners[i, 0] and corners[i, 1] lie below 192. `partners`: row i starts with i itself, names distinct orbitals whose boxes intersect box i (every component of o is above -32 and below 32), and has its -1 entries only after all others.
All inputs are finite; a program needn't handle non-finite values.
Results may differ from a plain program's by a relative error of at most 0.0003.
Values may be sent and summed in bfloat16 or wider, within the bound.
A program may use at most 64 MiB of HBM per device.

v0:
```python
import math
import jax
import jax.numpy as jnp
from jax import lax
from jax.sharding import PartitionSpec as P

G = 192
ZDEV = 12
PB = 4


def passed_along(array, axis, by):
    size = lax.axis_size(axis)
    return lax.ppermute(array, axis, [(i, (i + by) % size) for i in range(size)])


def wrapped(deltas, lengths):
    halfway = lengths // 2
    return jnp.mod(deltas + halfway, lengths) - halfway


def edge_shifter(offsets, box_edge):
    row_ids = lax.broadcasted_iota(jnp.int32, (offsets.shape[0], box_edge, box_edge), 1)
    col_ids = lax.broadcasted_iota(jnp.int32, (offsets.shape[0], box_edge, box_edge), 2)
    return (col_ids == row_ids + offsets[:, None, None]).astype(jnp.bfloat16)


def plane_shifter(offsets_b, offsets_c, box_edge):
    plane = box_edge * box_edge
    source = lax.broadcasted_iota(jnp.int32, (offsets_b.shape[0], plane, plane), 1)
    target = lax.broadcasted_iota(jnp.int32, (offsets_b.shape[0], plane, plane), 2)
    match_b = source // box_edge == target // box_edge + offsets_b[:, None, None]
    match_c = jnp.mod(source, box_edge) == jnp.mod(target, box_edge) + offsets_c[:, None, None]
    return (match_b & match_c).astype(jnp.bfloat16)


def place_boxes(orbital_boxes, offsets, box_edge):
    stride_along_first = edge_shifter(offsets[:, 0], box_edge)
    displaced_density = jnp.einsum(
        "rkd,rdw->rkw", stride_along_first, orbital_boxes, preferred_element_type=jnp.float32
    ).astype(jnp.bfloat16)
    step_plane = plane_shifter(offsets[:, 1], offsets[:, 2], box_edge)
    return jnp.einsum(
        "pam,pmn->pan", displaced_density, step_plane, preferred_element_type=jnp.float32
    )


def fourier_tables(box_edge):
    grid_ids = jnp.arange(box_edge, dtype=jnp.int32)
    phases = jnp.mod(grid_ids[:, None] * grid_ids[None, :], box_edge)
    angles = phases.astype(jnp.float32) * (2.0 * math.pi / box_edge)
    plane_ids = jnp.arange(box_edge * box_edge, dtype=jnp.int32)
    outer_ids = plane_ids // box_edge
    inner_ids = jnp.mod(plane_ids, box_edge)
    plane_phases = jnp.mod(
        outer_ids[:, None] * outer_ids[None, :] + inner_ids[:, None] * inner_ids[None, :], box_edge
    )
    plane_angles = plane_phases.astype(jnp.float32) * (2.0 * math.pi / box_edge)
    return (jnp.cos(angles), jnp.sin(angles), jnp.cos(plane_angles), jnp.sin(plane_angles))


def edge_rotation(values, matrix):
    return jnp.einsum("ka,pam->pkm", matrix, values, precision=lax.Precision.HIGHEST)


def plane_turn(values, table):
    return jnp.einsum("pam,mn->pan", values, table, precision=lax.Precision.HIGHEST)


def poisson(density, kernel, tables):
    cosine, sine, plane_cos, plane_sin = tables
    plane_real = plane_turn(density, plane_cos)
    plane_imag = -plane_turn(density, plane_sin)
    real_part = edge_rotation(plane_real, cosine) + edge_rotation(plane_imag, sine)
    imag_part = edge_rotation(plane_imag, cosine) - edge_rotation(plane_real, sine)
    real_part = real_part * kernel[None]
    imag_part = imag_part * kernel[None]
    back_real = edge_rotation(real_part, cosine) - edge_rotation(imag_part, sine)
    back_imag = edge_rotation(imag_part, cosine) + edge_rotation(real_part, sine)
    result = plane_turn(back_real, plane_cos) - plane_turn(back_imag, plane_sin)
    box_edge = density.shape[1]
    return result / float(box_edge**3)


def body(orbitals, corners, partners, kernel):
    own_count = orbitals.shape[0]
    box_edge = orbitals.shape[1]
    plane = box_edge * box_edge
    slab_count = lax.axis_size("slab")
    orb_count = lax.axis_size("orb")
    group_size = own_count * orb_count
    slab_position = lax.axis_index("slab")
    halo_depth = (ZDEV + box_edge - 2) // ZDEV
    gathered = lax.all_gather(orbitals, "orb", axis=0, tiled=True)
    lower = [gathered]
    upper = [gathered]
    for _ in range(halo_depth):
        lower.append(passed_along(lower[-1], "slab", 1))
        upper.append(passed_along(upper[-1], "slab", -1))
    nearby = jnp.concatenate(lower[::-1] + upper[1:], axis=0)
    rep_count = lax.axis_size("rep")
    rep_index = lax.axis_index("rep")
    half_slots = partners.shape[1] // rep_count
    chosen = lax.dynamic_index_in_dim(
        partners.reshape(own_count, half_slots, rep_count), rep_index, 2, keepdims=False
    )
    first_own = (slab_position * orb_count + lax.axis_index("orb")) * own_count
    owner_ids = jnp.repeat(jnp.arange(own_count, dtype=jnp.int32), half_slots)
    flat_ids = chosen.reshape(own_count * half_slots)
    usable = (flat_ids >= 0).astype(jnp.float32)
    safe_ids = jnp.maximum(flat_ids, 0)
    neighbour_slab = safe_ids // group_size
    slab_step = jnp.mod(neighbour_slab - slab_position + halo_depth, slab_count) - halo_depth
    pool_rows = (slab_step + halo_depth) * group_size + jnp.mod(safe_ids, group_size)
    lengths = jnp.array([G, G, ZDEV * slab_count], jnp.int32)
    own_corners = jnp.take(corners, first_own + owner_ids, axis=0, mode="clip")
    partner_corners = jnp.take(corners, safe_ids, axis=0, mode="clip")
    offsets = wrapped(own_corners - partner_corners, lengths)
    tables = fourier_tables(box_edge)
    block_size = PB
    block_count = own_count * half_slots // block_size

    def block_work(block_index, carry):
        exchange, energy = carry
        first_pair = block_index * block_size
        owner_slot = first_pair // half_slots
        slots = lax.dynamic_slice_in_dim(pool_rows, first_pair, block_size)
        block_offsets = lax.dynamic_slice_in_dim(offsets, first_pair, block_size, 0)
        block_usable = lax.dynamic_slice_in_dim(usable, first_pair, block_size)

        def active(anchor):
            orbital_boxes = jnp.take(nearby, slots, axis=0, mode="clip")
            shifted = (
                place_boxes(orbital_boxes, block_offsets, box_edge) * block_usable[:, None, None]
            )
            centre = lax.dynamic_index_in_dim(orbitals, owner_slot, 0, keepdims=False).astype(
                jnp.float32
            )
            density = centre[None] * shifted
            potential = poisson(density, kernel, tables)
            return (jnp.sum(potential * shifted, axis=0), jnp.sum(density * potential))

        def skipped(anchor):
            return (jnp.zeros((box_edge, plane), jnp.float32), jnp.zeros((), jnp.float32))

        pair_term, energy_part = lax.cond(jnp.sum(block_usable) > 0.0, active, skipped, first_pair)
        previous = lax.dynamic_index_in_dim(exchange, owner_slot, 0, keepdims=False)
        exchange = lax.dynamic_update_index_in_dim(exchange, previous - pair_term, owner_slot, 0)
        return (exchange, energy + energy_part)

    start_state = (jnp.zeros((own_count, box_edge, plane), jnp.float32), jnp.zeros((), jnp.float32))
    exchange, energy = lax.fori_loop(0, block_count, block_work, start_state)
    exchange_total, replica_energy = lax.psum((exchange, energy), "rep")
    energy_all = lax.psum(replica_energy, ("slab", "orb"))
    orbital_total = own_count * slab_count * orb_count
    exchange_energy = -energy_all / (2.0 * orbital_total * box_edge**3)
    return (exchange_total, exchange_energy.reshape(1))


def solution(mesh):
    in_specs = (
        P(("grp", "slab", "orb"), None, None),
        P("grp", None),
        P(("grp", "slab", "orb"), None),
        P(),
    )
    out_specs = (P(("grp", "slab", "orb"), None, None), P("grp"))
    return jax.shard_map(body, mesh=mesh, in_specs=in_specs, out_specs=out_specs, check_vma=False)
```

profile of v0, /device:TPU:0, one launch (start us, length us, event | category | flops | bytes accessed | tf_op | source)
XLA Modules:
  0.0 167.7 jit_solution(17566683294554462132)
XLA Ops:
  7.2 6.1 %all_gather.3 = bf16[2,32,1024]{2,1,0:T(8,128)(2,1)S(1)} all-gather(bf16[1,32,1024]{2,1,0:T(8,128)(2,1)} %param.9), channel_id=1, replica_groups=mesh['grp'=2,'slab'=4,'orb'=2,'rep'=2] {'orb'}, dimensions={0}, use_global_device_ids=true | all-gather | bytes 196608 | tf_op jit(solution)/shard_map/all_gather | solution.py:94
  13.3 2.1 %collective-permute-start = (bf16[2,32,1024]{2,1,0:T(8,128)(2,1)S(1)}, bf16[2,32,1024]{2,1,0:T(8,128)(2,1)S(1)}, u32[]{:S(2)}, u32[]{:S(2)}) collective-permute-start(bf16[2,32,1024]{2,1,0:T(8,128)(2,1)S(1)} %all_gather.3), channel_id=1, source_target_pairs={{0,4},{4,8},{8,12},{12,0},{1,5},{5,9},{9,13},{13,1},{2,6},{6,10},{... | collective-permute-start | bytes 393224 | tf_op jit(solution)/shard_map/ppermute | solution.py:14
  15.4 2.0 %collective-permute-start.3 = (bf16[2,32,1024]{2,1,0:T(8,128)(2,1)S(1)}, bf16[2,32,1024]{2,1,0:T(8,128)(2,1)S(1)}, u32[]{:S(2)}, u32[]{:S(2)}) collective-permute-start(bf16[2,32,1024]{2,1,0:T(8,128)(2,1)S(1)} %all_gather.3), channel_id=1, source_target_pairs={{0,12},{4,0},{8,4},{12,8},{1,13},{5,1},{9,5},{13,9},{2,14},{6,2},{... | collective-permute-start | bytes 393224 | tf_op jit(solution)/shard_map/ppermute | solution.py:14
  17.4 0.8 copy.13
  18.2 0.5 broadcast.390
  18.7 1.3 reduce.13
  20.0 0.1 reshape.92
  20.1 0.2 shift-right-logical_reduce_fusion
  20.4 0.6 gather_fusion.2
  20.9 0.6 gather_fusion.1
  21.5 0.2 fusion.72
  21.7 0.1 collective-permute-start.1
  21.7 0.8 fusion.67
  22.6 3.9 %collective-permute-start.4 = (bf16[2,32,1024]{2,1,0:T(8,128)(2,1)S(1)}, bf16[2,32,1024]{2,1,0:T(8,128)(2,1)S(1)}, u32[]{:S(2)}, u32[]{:S(2)}) collective-permute-start(bf16[2,32,1024]{2,1,0:T(8,128)(2,1)S(1)} %collective-permute-done.3), channel_id=1, source_target_pairs={{0,12},{4,0},{8,4},{12,8},{1,13},{5,1},{9,5},{13,9},{2,14},{6,2},{... | collective-permute-start | bytes 393224 | tf_op jit(solution)/shard_map/ppermute | solution.py:14
  26.4 2.5 %collective-permute-done.1 = bf16[2,32,1024]{2,1,0:T(8,128)(2,1)S(1)} collective-permute-done((bf16[2,32,1024]{2,1,0:T(8,128)(2,1)S(1)}, bf16[2,32,1024]{2,1,0:T(8,128)(2,1)S(1)}, u32[]{:S(2)}, u32[]{:S(2)}) %collective-permute-start.1) | collective-permute-done | bytes 131104 | tf_op jit(solution)/shard_map/ppermute | solution.py:14
  28.9 0.1 copy.15
  29.0 0.2 convert_reduce_fusion
  29.2 4.9 %collective-permute-start.5 = (bf16[2,32,1024]{2,1,0:T(8,128)(2,1)S(1)}, bf16[2,32,1024]{2,1,0:T(8,128)(2,1)S(1)}, u32[]{:S(2)}, u32[]{:S(2)}) collective-permute-start(bf16[2,32,1024]{2,1,0:T(8,128)(2,1)S(1)} %collective-permute-done.4), channel_id=1, source_target_pairs={{0,12},{4,0},{8,4},{12,8},{1,13},{5,1},{9,5},{13,9},{2,14},{6,2},{... | collective-permute-start | bytes 393224 | tf_op jit(solution)/shard_map/ppermute | solution.py:14
  34.1 2.7 %collective-permute-done.2 = bf16[2,32,1024]{2,1,0:T(8,128)(2,1)S(1)} collective-permute-done((bf16[2,32,1024]{2,1,0:T(8,128)(2,1)S(1)}, bf16[2,32,1024]{2,1,0:T(8,128)(2,1)S(1)}, u32[]{:S(2)}, u32[]{:S(2)}) %collective-permute-start.2) | collective-permute-done | bytes 131104 | tf_op jit(solution)/shard_map/ppermute | solution.py:14
  36.9 0.3 collective-permute-done.5
  37.3 93.5 %while.20 = (s32[]{:T(128)}, f32[1,32,1024]{2,1,0:T(8,128)S(1)}, f32[]{:T(128)}, f32[12]{0:T(128)S(1)}, bf16[1,32,1024]{2,1,0:T(8,128)(2,1)}, /*index=5*/s32[12,...) while((s32[]{:T(128)}, f32[1,32,1024]{2,1,0:T(8,128)S(1)}, ...), condition=%wide.region_6.7_spmd.clone.clone.clone, body=%wide.region_0.6_spmd.clone.clone.clone.sunk | while | flops 7178883072 | bytes 56513292 | solution.py:152
  37.4 0.8 fusion.96
  38.8 3.7 %fusion.97 = f32[1024,1024]{1,0:T(8,128)} fusion(s32[1024]{0:T(1024)S(1)} %get-tuple-element.785, s32[1024]{0:T(1024)S(1)} %get-tuple-element.784), kind=kLoop, calls=%fused_computation.81.clone.1 | loop fusion | flops 16777216 | bytes 4202496 | tf_op jit(solution)/shard_map/mul | solution.py:58
  42.5 77.8 %conditional.5 = (f32[32,1024]{1,0:T(8,128)S(1)}, f32[]{:T(128)}) conditional(s32[]{:T(128)} %convert_element_type.98, () %tuple.97, (bf16[1,32,1024]{2,1,0:T(8,128)(2,1)S(1)}, s32[12,3]{0,1:T(4,128)S(1)}, s32[]{:T(128)}, s32[12]{0:T(128)S(1)}, bf16[14,32,1024]{2,1,0:T(8,128)(2,1)S(1)}, /*index=5*/f32[4]{0:T(128)S(1)}, f32[1024,1024]{1,0:T(8,128)}, ...), branch_computations={%region_2.2_spmd, %region_3.5_spmd.clone} | conditional | flops 7162058752 | bytes 51126648 | solution.py:146
  42.5 0.1 dynamic_slice.48
  42.6 0.1 constant_dynamic-slice_fusion
  42.7 0.6 gather_fusion
  43.3 4.2 %fusion.38 = f32[4,32,1024]{2,1,0:T(8,128)S(1)} fusion(s32[4]{0:T(128)S(1)} %get-tuple-element.652, s32[1024]{0:T(1024)S(1)} %get-tuple-element.655, s32[1024]{0:T(1024)S(1)} %get-tuple-element.656, s32[4]{0:T(128)S(1)} %get-tuple-element.653, s32[1024]{0:T(1024)S(1)} %get-tuple-element.654, s32[1024]{0:T(1024)S(1)} %get-tuple-element.657, ...), kind=kOutput, calls=%fused_computation.44 | convolution fusion | flops 314843136 | bytes 804928 | tf_op jit(solution)/shard_map/while/body/eval_jaxpr/cond/branch_1_fun/pam,pmn->pan/dot_general | solution.py:43
  47.5 17.6 %fusion.31 = f32[4,32,1024]{2,1,0:T(8,128)S(1)} fusion(f32[1024,1024]{1,0:T(8,128)} %get-tuple-element.609, f32[4,32,1024]{2,1,0:T(8,128)S(1)} %fusion.38, f32[32,1024]{1,0:T(8,128)S(1)} %bitcast_convert_fusion), kind=kOutput, calls=%fused_computation.33 | convolution fusion | flops 1610874880 | bytes 5373952 | tf_op jit(solution)/shard_map/while/body/eval_jaxpr/cond/branch_1_fun/pam,mn->pan/dot_general | solution.py:67
  65.1 16.2 %fusion.26 = f32[4,32,1024]{2,1,0:T(8,128)S(1)} fusion(f32[1024,1024]{1,0:T(8,128)S(1)} %copy-done, f32[4,32,1024]{2,1,0:T(8,128)S(1)} %fusion.38, f32[32,1024]{1,0:T(8,128)S(1)} %bitcast_convert_fusion), kind=kOutput, calls=%fused_computation.28 | convolution fusion | flops 1610743808 | bytes 5373952 | tf_op jit(solution)/shard_map/while/body/eval_jaxpr/cond/branch_1_fun/pam,mn->pan/dot_general | solution.py:67
  81.3 0.7 fusion.50
  82.0 0.7 fusion.37
  82.7 0.6 fusion.48
  83.3 0.7 fusion.35
  84.0 0.7 fusion.47
  84.7 0.7 fusion.32
  85.4 0.7 fusion.49
  86.0 0.7 fusion.33
  86.7 16.2 %fusion.25 = f32[4,32,1024]{2,1,0:T(8,128)S(1)} fusion(f32[4,32,1024]{2,1,0:T(8,128)S(1)} %fusion.33, f32[1024,1024]{1,0:T(8,128)S(1)} %copy-done), kind=kOutput, calls=%fused_computation.27 | convolution fusion | flops 1610612736 | bytes 5242880 | tf_op jit(solution)/shard_map/while/body/eval_jaxpr/cond/branch_1_fun/pam,mn->pan/dot_general | solution.py:67
  102.9 16.7 %multiply_reduce_fusion = (f32[]{:T(128)}, f32[32,1024]{1,0:T(8,128)S(1)}) fusion(f32[4,32,1024]{2,1,0:T(8,128)S(1)} %fusion.38, f32[32,1024]{1,0:T(8,128)S(1)} %bitcast_convert_fusion, f32[4,32,1024]{2,1,0:T(8,128)S(1)} %fusion.25, f32[4,32,1024]{2,1,0:T(8,128)S(1)} %fusion.32, f32[1024,1024]{1,0:T(8,128)S(1)} %copy-done), kind=kOutput, calls=%fused_computation.46 | convolution fusion | flops 1611497472 | bytes 6029316 | tf_op jit(solution)/shard_map/while/body/eval_jaxpr/cond/branch_1_fun/pam,mn->pan/dot_general | solution.py:67
  120.4 0.8 fusion.96
  121.8 3.7 %fusion.97 = f32[1024,1024]{1,0:T(8,128)} fusion(s32[1024]{0:T(1024)S(1)} %get-tuple-element.785, s32[1024]{0:T(1024)S(1)} %get-tuple-element.784), kind=kLoop, calls=%fused_computation.81.clone.1 | loop fusion | flops 16777216 | bytes 4202496 | tf_op jit(solution)/shard_map/mul | solution.py:58
  125.6 0.8 fusion.96
  127.1 3.7 %fusion.97 = f32[1024,1024]{1,0:T(8,128)} fusion(s32[1024]{0:T(1024)S(1)} %get-tuple-element.785, s32[1024]{0:T(1024)S(1)} %get-tuple-element.784), kind=kLoop, calls=%fused_computation.81.clone.1 | loop fusion | flops 16777216 | bytes 4202496 | tf_op jit(solution)/shard_map/mul | solution.py:58
  130.9 0.6 copy-done.2
  131.5 3.7 %psum.22 = f32[]{:T(128)} all-reduce(f32[]{:T(128)} %get-tuple-element.447), channel_id=1, replica_groups=mesh['grp'=2,'slab'=4,'orb'=2,'rep'=2] {'rep'}, use_global_device_ids=true, to_apply=%region_8.9 | all-reduce | flops 1 | bytes 8 | tf_op jit(solution)/shard_map/psum | solution.py:153
  135.2 22.3 %psum.23 = f32[]{:T(128)} all-reduce(f32[]{:T(128)} %psum.22), channel_id=1, replica_groups=mesh['grp'=2,'slab'=4,'orb'=2,'rep'=2] {'slab','orb'}, use_global_device_ids=true, to_apply=%region_9.10 | all-reduce | flops 1 | bytes 8 | tf_op jit(solution)/shard_map/psum | solution.py:154
  158.2 1.6 copy.38
  (50 shorter events, 0.5 us)
Async XLA Ops:
  7.2 151.0 %all-reduce.2.cloned.1.call-start = ((), (), s32[]{:S(2)}) async-start(), calls=%async_computation | async-start | bytes 262144 | tf_op jit(solution)/shard_map/psum | solution.py:153
  13.3 8.3 %collective-permute-start = (bf16[2,32,1024]{2,1,0:T(8,128)(2,1)S(1)}, bf16[2,32,1024]{2,1,0:T(8,128)(2,1)S(1)}, u32[]{:S(2)}, u32[]{:S(2)}) collective-permute-start(bf16[2,32,1024]{2,1,0:T(8,128)(2,1)S(1)} %all_gather.3), channel_id=1, source_target_pairs={{0,4},{4,8},{8,12},{12,0},{1,5},{5,9},{9,13},{13,1},{2,6},{6,10},{... | collective-permute-start | bytes 393224 | tf_op jit(solution)/shard_map/ppermute | solution.py:14
  15.4 7.2 %collective-permute-start.3 = (bf16[2,32,1024]{2,1,0:T(8,128)(2,1)S(1)}, bf16[2,32,1024]{2,1,0:T(8,128)(2,1)S(1)}, u32[]{:S(2)}, u32[]{:S(2)}) collective-permute-start(bf16[2,32,1024]{2,1,0:T(8,128)(2,1)S(1)} %all_gather.3), channel_id=1, source_target_pairs={{0,12},{4,0},{8,4},{12,8},{1,13},{5,1},{9,5},{13,9},{2,14},{6,2},{... | collective-permute-start | bytes 393224 | tf_op jit(solution)/shard_map/ppermute | solution.py:14
  21.7 7.2 %collective-permute-start.1 = (bf16[2,32,1024]{2,1,0:T(8,128)(2,1)S(1)}, bf16[2,32,1024]{2,1,0:T(8,128)(2,1)S(1)}, u32[]{:S(2)}, u32[]{:S(2)}) collective-permute-start(bf16[2,32,1024]{2,1,0:T(8,128)(2,1)S(1)} %collective-permute-done), channel_id=1, source_target_pairs={{0,4},{4,8},{8,12},{12,0},{1,5},{5,9},{9,13},{13,1},{2,6},{6,10},{... | collective-permute-start | bytes 393224 | tf_op jit(solution)/shard_map/ppermute | solution.py:14
  22.6 6.7 %collective-permute-start.4 = (bf16[2,32,1024]{2,1,0:T(8,128)(2,1)S(1)}, bf16[2,32,1024]{2,1,0:T(8,128)(2,1)S(1)}, u32[]{:S(2)}, u32[]{:S(2)}) collective-permute-start(bf16[2,32,1024]{2,1,0:T(8,128)(2,1)S(1)} %collective-permute-done.3), channel_id=1, source_target_pairs={{0,12},{4,0},{8,4},{12,8},{1,13},{5,1},{9,5},{13,9},{2,14},{6,2},{... | collective-permute-start | bytes 393224 | tf_op jit(solution)/shard_map/ppermute | solution.py:14
  28.9 7.9 %collective-permute-start.2 = (bf16[2,32,1024]{2,1,0:T(8,128)(2,1)S(1)}, bf16[2,32,1024]{2,1,0:T(8,128)(2,1)S(1)}, u32[]{:S(2)}, u32[]{:S(2)}) collective-permute-start(bf16[2,32,1024]{2,1,0:T(8,128)(2,1)S(1)} %collective-permute-done.1), channel_id=1, source_target_pairs={{0,4},{4,8},{8,12},{12,0},{1,5},{5,9},{9,13},{13,1},{2,6},{6,10},{... | collective-permute-start | bytes 393224 | tf_op jit(solution)/shard_map/ppermute | solution.py:14
  29.2 8.0 %collective-permute-start.5 = (bf16[2,32,1024]{2,1,0:T(8,128)(2,1)S(1)}, bf16[2,32,1024]{2,1,0:T(8,128)(2,1)S(1)}, u32[]{:S(2)}, u32[]{:S(2)}) collective-permute-start(bf16[2,32,1024]{2,1,0:T(8,128)(2,1)S(1)} %collective-permute-done.4), channel_id=1, source_target_pairs={{0,12},{4,0},{8,4},{12,8},{1,13},{5,1},{9,5},{13,9},{2,14},{6,2},{... | collective-permute-start | bytes 393224 | tf_op jit(solution)/shard_map/ppermute | solution.py:14
  37.3 5.2 %copy-start.1 = (f32[32,1024]{1,0:T(8,128)S(1)}, f32[32,1024]{1,0:T(8,128)}, u32[]{:S(2)}) copy-start(f32[32,1024]{1,0:T(8,128)} %get-tuple-element.783) | copy-start | bytes 393220 | tf_op jit(solution)/shard_map/while
  37.3 5.2 %copy-start.3 = (bf16[1,32,1024]{2,1,0:T(8,128)(2,1)S(1)}, bf16[1,32,1024]{2,1,0:T(8,128)(2,1)}, u32[]{:S(2)}) copy-start(bf16[1,32,1024]{2,1,0:T(8,128)(2,1)} %get-tuple-element.779) | copy-start | bytes 196612 | tf_op jit(solution)/shard_map/while
  47.5 17.6 %copy-start = (f32[1024,1024]{1,0:T(8,128)S(1)}, f32[1024,1024]{1,0:T(8,128)}, u32[]{:S(2)}) copy-start(f32[1024,1024]{1,0:T(8,128)} %get-tuple-element.609) | copy-start | bytes 12582916 | tf_op jit(solution)/shard_map/while/body/eval_jaxpr/cond
  120.3 5.2 %copy-start.1 = (f32[32,1024]{1,0:T(8,128)S(1)}, f32[32,1024]{1,0:T(8,128)}, u32[]{:S(2)}) copy-start(f32[32,1024]{1,0:T(8,128)} %get-tuple-element.783) | copy-start | bytes 393220 | tf_op jit(solution)/shard_map/while
  120.3 5.2 %copy-start.3 = (bf16[1,32,1024]{2,1,0:T(8,128)(2,1)S(1)}, bf16[1,32,1024]{2,1,0:T(8,128)(2,1)}, u32[]{:S(2)}) copy-start(bf16[1,32,1024]{2,1,0:T(8,128)(2,1)} %get-tuple-element.779) | copy-start | bytes 196612 | tf_op jit(solution)/shard_map/while
  125.6 5.2 %copy-start.1 = (f32[32,1024]{1,0:T(8,128)S(1)}, f32[32,1024]{1,0:T(8,128)}, u32[]{:S(2)}) copy-start(f32[32,1024]{1,0:T(8,128)} %get-tuple-element.783) | copy-start | bytes 393220 | tf_op jit(solution)/shard_map/while
  125.6 5.2 %copy-start.3 = (bf16[1,32,1024]{2,1,0:T(8,128)(2,1)S(1)}, bf16[1,32,1024]{2,1,0:T(8,128)(2,1)}, u32[]{:S(2)}) copy-start(bf16[1,32,1024]{2,1,0:T(8,128)(2,1)} %get-tuple-element.779) | copy-start | bytes 196612 | tf_op jit(solution)/shard_map/while
  130.9 0.7 copy-start.2
Sparse Core Ops, SparseCore 0:
  131.7 19.1 all-reduce.1
where the time goes:
time: 168 us
  matrix products  76.2 us (45%)
  blocking collectives  32.1 us (19%)
  other arithmetic  16.2 us (10%)
  between operations  15.9 us (9%)
  starting transfers between devices  12.9 us (8%)
  local copies, waits for them, and re-layouts  5.64 us (3%)
  waiting for transfers between devices  5.57 us (3%)
  loops' own time  3.13 us (2%)
    dot_general x4, matrix products, plane_turn(): jnp.einsum('pam,mn->pan', values, table, precision=lax.Precision.HIGHEST)  66.7 us
    psum x1, blocking collectives, body(): energy_all = lax.psum(replica_energy, ('slab', 'orb'))  22.3 us
    ppermute x6, starting transfers between devices, passed_along(): lax.ppermute(array, axis, [(i, (i + by) % size) for i in range(size)])  12.9 us
    mul x3, other arithmetic, fourier_tables(): plane_angles = plane_phases.astype(jnp.float32) * (2.0 * math.pi / box_edge)  11 us
    all_gather x1, blocking collectives, body(): gathered = lax.all_gather(orbitals, 'orb', axis=0, tiled=True)  6.14 us
    ppermute x6, waiting for transfers between devices, passed_along(): lax.ppermute(array, axis, [(i, (i + by) % size) for i in range(size)])  5.54 us
    dot_general x8, matrix products, edge_rotation(): jnp.einsum('ka,pam->pkm', matrix, values, precision=lax.Precision.HIGHEST)  5.3 us
    dot_general x1, matrix products, place_boxes(): jnp.einsum('pam,pmn->pan', displaced_density, step_plane, preferred_eleme...  4.2 us
  transfers between devices with their start and end apart: 7, of which 4 were waited for; matrix products, arithmetic and copies ran while one was open for 3% of the time, Pallas kernels for 0%

commit v1 on v0

--- a/solution.py
+++ b/solution.py
@@ -151,7 +151,7 @@
     start_state = (jnp.zeros((own_count, box_edge, plane), jnp.float32), jnp.zeros((), jnp.float32))
     exchange, energy = lax.fori_loop(0, block_count, block_work, start_state)
     exchange_total, replica_energy = lax.psum((exchange, energy), "rep")
-    energy_all = lax.psum(replica_energy, ("slab", "orb"))
+    energy_all = jnp.sum(lax.all_gather(replica_energy, ("slab", "orb")), axis=0)
     orbital_total = own_count * slab_count * orb_count
     exchange_energy = -energy_all / (2.0 * orbital_total * box_edge**3)
     return (exchange_total, exchange_energy.reshape(1))

time: 168 us -> 170 us (1.012)
  local copies, waits for them, and re-layouts: 5.64 us -> 7.54 us
    psum x1 -> x0, blocking collectives: 22.3 us -> none  [body(): energy_all = lax.psum(replica_energy, ('slab', 'orb'))]
    unnamed x0 -> x1, blocking collectives: none -> 21.7 us
    unnamed x12 -> x17, local copies, waits for them, and re-layouts: 3.64 us -> 5.54 us
  transfers between devices with their start and end apart: 7 -> 7, of which waited for: 4 -> 4; matrix products, arithmetic and copies ran while one was open for 3% -> 5% of each run, Pallas kernels for 0% -> 0%
where the time goes in v1:
time: 170 us
  matrix products  76.2 us (45%)
  blocking collectives  31.4 us (18%)
  other arithmetic  16.8 us (10%)
  between operations  16 us (9%)
  starting transfers between devices  12.9 us (8%)
  local copies, waits for them, and re-layouts  7.54 us (4%)
  waiting for transfers between devices  5.58 us (3%)
  loops' own time  3.13 us (2%)
    dot_general x4, matrix products, plane_turn(): jnp.einsum('pam,mn->pan', values, table, precision=lax.Precision.HIGHEST)  66.7 us
    unnamed x1, blocking collectives  21.7 us
    ppermute x6, starting transfers between devices, passed_along(): lax.ppermute(array, axis, [(i, (i + by) % size) for i in range(size)])  12.9 us
    mul x3, other arithmetic, fourier_tables(): plane_angles = plane_phases.astype(jnp.float32) * (2.0 * math.pi / box_edge)  11 us
    all_gather x1, blocking collectives, body(): gathered = lax.all_gather(orbitals, 'orb', axis=0, tiled=True)  6.14 us
    unnamed x17, local copies, waits for them, and re-layouts  5.54 us
    ppermute x6, waiting for transfers between devices, passed_along(): lax.ppermute(array, axis, [(i, (i + by) % size) for i in range(size)])  5.54 us
    dot_general x8, matrix products, edge_rotation(): jnp.einsum('ka,pam->pkm', matrix, values, precision=lax.Precision.HIGHEST)  5.3 us
  transfers between devices with their start and end apart: 7, of which 4 were waited for; matrix products, arithmetic and copies ran while one was open for 5% of the time, Pallas kernels for 0%

profile of v1, /device:TPU:0, one launch (start us, length us, event | category | flops | bytes accessed | tf_op | source)
XLA Modules:
  0.0 169.6 jit_solution(17511443994075038303)
XLA Ops:
  7.2 6.1 %all_gather.9 = bf16[2,32,1024]{2,1,0:T(8,128)(2,1)S(1)} all-gather(bf16[1,32,1024]{2,1,0:T(8,128)(2,1)} %param.9), channel_id=1, replica_groups=mesh['grp'=2,'slab'=4,'orb'=2,'rep'=2] {'orb'}, dimensions={0}, use_global_device_ids=true | all-gather | bytes 196608 | tf_op jit(solution)/shard_map/all_gather | solution.py:94
  13.3 2.1 %collective-permute-start = (bf16[2,32,1024]{2,1,0:T(8,128)(2,1)S(1)}, bf16[2,32,1024]{2,1,0:T(8,128)(2,1)S(1)}, u32[]{:S(2)}, u32[]{:S(2)}) collective-permute-start(bf16[2,32,1024]{2,1,0:T(8,128)(2,1)S(1)} %all_gather.9), channel_id=1, source_target_pairs={{0,4},{4,8},{8,12},{12,0},{1,5},{5,9},{9,13},{13,1},{2,6},{6,10},{... | collective-permute-start | bytes 393224 | tf_op jit(solution)/shard_map/ppermute | solution.py:14
  15.4 2.0 %collective-permute-start.3 = (bf16[2,32,1024]{2,1,0:T(8,128)(2,1)S(1)}, bf16[2,32,1024]{2,1,0:T(8,128)(2,1)S(1)}, u32[]{:S(2)}, u32[]{:S(2)}) collective-permute-start(bf16[2,32,1024]{2,1,0:T(8,128)(2,1)S(1)} %all_gather.9), channel_id=1, source_target_pairs={{0,12},{4,0},{8,4},{12,8},{1,13},{5,1},{9,5},{13,9},{2,14},{6,2},{... | collective-permute-start | bytes 393224 | tf_op jit(solution)/shard_map/ppermute | solution.py:14
  17.4 0.8 copy.13
  18.2 0.5 broadcast.391
  18.7 1.3 reduce.14
  20.0 0.1 reshape.92
  20.1 0.2 shift-right-logical_reduce_fusion
  20.4 0.6 gather_fusion.2
  20.9 0.6 gather_fusion.1
  21.5 0.2 fusion.72
  21.7 0.8 fusion.67
  22.6 3.9 %collective-permute-start.4 = (bf16[2,32,1024]{2,1,0:T(8,128)(2,1)S(1)}, bf16[2,32,1024]{2,1,0:T(8,128)(2,1)S(1)}, u32[]{:S(2)}, u32[]{:S(2)}) collective-permute-start(bf16[2,32,1024]{2,1,0:T(8,128)(2,1)S(1)} %collective-permute-done.3), channel_id=1, source_target_pairs={{0,12},{4,0},{8,4},{12,8},{1,13},{5,1},{9,5},{13,9},{2,14},{6,2},{... | collective-permute-start | bytes 393224 | tf_op jit(solution)/shard_map/ppermute | solution.py:14
  26.4 2.5 %collective-permute-done.1 = bf16[2,32,1024]{2,1,0:T(8,128)(2,1)S(1)} collective-permute-done((bf16[2,32,1024]{2,1,0:T(8,128)(2,1)S(1)}, bf16[2,32,1024]{2,1,0:T(8,128)(2,1)S(1)}, u32[]{:S(2)}, u32[]{:S(2)}) %collective-permute-start.1) | collective-permute-done | bytes 131104 | tf_op jit(solution)/shard_map/ppermute | solution.py:14
  28.9 0.1 copy.15
  29.0 0.2 convert_reduce_fusion
  29.2 4.9 %collective-permute-start.5 = (bf16[2,32,1024]{2,1,0:T(8,128)(2,1)S(1)}, bf16[2,32,1024]{2,1,0:T(8,128)(2,1)S(1)}, u32[]{:S(2)}, u32[]{:S(2)}) collective-permute-start(bf16[2,32,1024]{2,1,0:T(8,128)(2,1)S(1)} %collective-permute-done.4), channel_id=1, source_target_pairs={{0,12},{4,0},{8,4},{12,8},{1,13},{5,1},{9,5},{13,9},{2,14},{6,2},{... | collective-permute-start | bytes 393224 | tf_op jit(solution)/shard_map/ppermute | solution.py:14
  34.1 2.7 %collective-permute-done.2 = bf16[2,32,1024]{2,1,0:T(8,128)(2,1)S(1)} collective-permute-done((bf16[2,32,1024]{2,1,0:T(8,128)(2,1)S(1)}, bf16[2,32,1024]{2,1,0:T(8,128)(2,1)S(1)}, u32[]{:S(2)}, u32[]{:S(2)}) %collective-permute-start.2) | collective-permute-done | bytes 131104 | tf_op jit(solution)/shard_map/ppermute | solution.py:14
  36.9 0.3 collective-permute-done.5
  37.3 93.5 %while.20 = (s32[]{:T(128)}, f32[1,32,1024]{2,1,0:T(8,128)S(1)}, f32[]{:T(128)}, f32[12]{0:T(128)S(1)}, bf16[1,32,1024]{2,1,0:T(8,128)(2,1)}, /*index=5*/s32[12,...) while((s32[]{:T(128)}, f32[1,32,1024]{2,1,0:T(8,128)S(1)}, ...), condition=%wide.region_6.7_spmd.clone.clone.clone, body=%wide.region_0.6_spmd.clone.clone.clone.sunk | while | flops 7178883072 | bytes 56513292 | solution.py:152
  37.4 0.8 fusion.96
  38.8 3.7 %fusion.97 = f32[1024,1024]{1,0:T(8,128)} fusion(s32[1024]{0:T(1024)S(1)} %get-tuple-element.785, s32[1024]{0:T(1024)S(1)} %get-tuple-element.784), kind=kLoop, calls=%fused_computation.81.clone.1 | loop fusion | flops 16777216 | bytes 4202496 | tf_op jit(solution)/shard_map/mul | solution.py:58
  42.5 77.8 %conditional.5 = (f32[32,1024]{1,0:T(8,128)S(1)}, f32[]{:T(128)}) conditional(s32[]{:T(128)} %convert_element_type.98, () %tuple.97, (bf16[1,32,1024]{2,1,0:T(8,128)(2,1)S(1)}, s32[12,3]{0,1:T(4,128)S(1)}, s32[]{:T(128)}, s32[12]{0:T(128)S(1)}, bf16[14,32,1024]{2,1,0:T(8,128)(2,1)S(1)}, /*index=5*/f32[4]{0:T(128)S(1)}, f32[1024,1024]{1,0:T(8,128)}, ...), branch_computations={%region_2.2_spmd, %region_3.5_spmd.clone} | conditional | flops 7162058752 | bytes 51126648 | solution.py:146
  42.7 0.6 gather_fusion
  43.3 4.2 %fusion.38 = f32[4,32,1024]{2,1,0:T(8,128)S(1)} fusion(s32[4]{0:T(128)S(1)} %get-tuple-element.652, s32[1024]{0:T(1024)S(1)} %get-tuple-element.655, s32[1024]{0:T(1024)S(1)} %get-tuple-element.656, s32[4]{0:T(128)S(1)} %get-tuple-element.653, s32[1024]{0:T(1024)S(1)} %get-tuple-element.654, s32[1024]{0:T(1024)S(1)} %get-tuple-element.657, ...), kind=kOutput, calls=%fused_computation.44 | convolution fusion | flops 314843136 | bytes 804928 | tf_op jit(solution)/shard_map/while/body/eval_jaxpr/cond/branch_1_fun/pam,pmn->pan/dot_general | solution.py:43
  47.5 17.6 %fusion.31 = f32[4,32,1024]{2,1,0:T(8,128)S(1)} fusion(f32[1024,1024]{1,0:T(8,128)} %get-tuple-element.609, f32[4,32,1024]{2,1,0:T(8,128)S(1)} %fusion.38, f32[32,1024]{1,0:T(8,128)S(1)} %bitcast_convert_fusion), kind=kOutput, calls=%fused_computation.33 | convolution fusion | flops 1610874880 | bytes 5373952 | tf_op jit(solution)/shard_map/while/body/eval_jaxpr/cond/branch_1_fun/pam,mn->pan/dot_general | solution.py:67
  65.2 16.2 %fusion.26 = f32[4,32,1024]{2,1,0:T(8,128)S(1)} fusion(f32[1024,1024]{1,0:T(8,128)S(1)} %copy-done, f32[4,32,1024]{2,1,0:T(8,128)S(1)} %fusion.38, f32[32,1024]{1,0:T(8,128)S(1)} %bitcast_convert_fusion), kind=kOutput, calls=%fused_computation.28 | convolution fusion | flops 1610743808 | bytes 5373952 | tf_op jit(solution)/shard_map/while/body/eval_jaxpr/cond/branch_1_fun/pam,mn->pan/dot_general | solution.py:67
  81.4 0.7 fusion.50
  82.0 0.7 fusion.37
  82.7 0.6 fusion.48
  83.4 0.7 fusion.35
  84.0 0.7 fusion.47
  84.7 0.7 fusion.32
  85.4 0.7 fusion.49
  86.0 0.7 fusion.33
  86.7 16.2 %fusion.25 = f32[4,32,1024]{2,1,0:T(8,128)S(1)} fusion(f32[4,32,1024]{2,1,0:T(8,128)S(1)} %fusion.33, f32[1024,1024]{1,0:T(8,128)S(1)} %copy-done), kind=kOutput, calls=%fused_computation.27 | convolution fusion | flops 1610612736 | bytes 5242880 | tf_op jit(solution)/shard_map/while/body/eval_jaxpr/cond/branch_1_fun/pam,mn->pan/dot_general | solution.py:67
  102.9 16.7 %multiply_reduce_fusion = (f32[]{:T(128)}, f32[32,1024]{1,0:T(8,128)S(1)}) fusion(f32[4,32,1024]{2,1,0:T(8,128)S(1)} %fusion.38, f32[32,1024]{1,0:T(8,128)S(1)} %bitcast_convert_fusion, f32[4,32,1024]{2,1,0:T(8,128)S(1)} %fusion.25, f32[4,32,1024]{2,1,0:T(8,128)S(1)} %fusion.32, f32[1024,1024]{1,0:T(8,128)S(1)} %copy-done), kind=kOutput, calls=%fused_computation.46 | convolution fusion | flops 1611497472 | bytes 6029316 | tf_op jit(solution)/shard_map/while/body/eval_jaxpr/cond/branch_1_fun/pam,mn->pan/dot_general | solution.py:67
  120.4 0.8 fusion.96
  121.9 3.7 %fusion.97 = f32[1024,1024]{1,0:T(8,128)} fusion(s32[1024]{0:T(1024)S(1)} %get-tuple-element.785, s32[1024]{0:T(1024)S(1)} %get-tuple-element.784), kind=kLoop, calls=%fused_computation.81.clone.1 | loop fusion | flops 16777216 | bytes 4202496 | tf_op jit(solution)/shard_map/mul | solution.py:58
  125.6 0.8 fusion.96
  127.1 3.7 %fusion.97 = f32[1024,1024]{1,0:T(8,128)} fusion(s32[1024]{0:T(1024)S(1)} %get-tuple-element.785, s32[1024]{0:T(1024)S(1)} %get-tuple-element.784), kind=kLoop, calls=%fused_computation.81.clone.1 | loop fusion | flops 16777216 | bytes 4202496 | tf_op jit(solution)/shard_map/mul | solution.py:58
  130.9 0.6 copy-done.2
  131.6 0.6 dynamic-slice
  132.2 3.6 %psum.15 = f32[1]{0:T(128)} all-reduce(f32[1]{0:T(128)} %bitcast.20), channel_id=1, replica_groups=mesh['grp'=2,'slab'=4,'orb'=2,'rep'=2] {'rep'}, use_global_device_ids=true, to_apply=%region_8.9 | all-reduce | flops 1 | bytes 8 | tf_op jit(solution)/shard_map/psum | solution.py:153
  135.8 1.3 dynamic-update-slice
  137.1 21.7 %all-reduce = f32[8]{0:T(128)S(1)} all-reduce(f32[8]{0:T(128)S(1)} %dynamic-update-slice), channel_id=1, replica_groups=mesh['grp'=2,'slab'=4,'orb'=2,'rep'=2] {'slab','orb'}, use_global_device_ids=true, to_apply=%add | all-reduce | flops 8 | bytes 64
  158.7 0.6 reduce_sum.48
  160.0 1.6 copy.39
  (56 shorter events, 0.7 us)
Async XLA Ops:
  7.2 152.8 %all-reduce.3.cloned.1.call-start = ((), (), s32[]{:S(2)}) async-start(), calls=%async_computation | async-start | bytes 262144 | tf_op jit(solution)/shard_map/psum | solution.py:153
  13.3 8.3 %collective-permute-start = (bf16[2,32,1024]{2,1,0:T(8,128)(2,1)S(1)}, bf16[2,32,1024]{2,1,0:T(8,128)(2,1)S(1)}, u32[]{:S(2)}, u32[]{:S(2)}) collective-permute-start(bf16[2,32,1024]{2,1,0:T(8,128)(2,1)S(1)} %all_gather.9), channel_id=1, source_target_pairs={{0,4},{4,8},{8,12},{12,0},{1,5},{5,9},{9,13},{13,1},{2,6},{6,10},{... | collective-permute-start | bytes 393224 | tf_op jit(solution)/shard_map/ppermute | solution.py:14
  15.4 7.2 %collective-permute-start.3 = (bf16[2,32,1024]{2,1,0:T(8,128)(2,1)S(1)}, bf16[2,32,1024]{2,1,0:T(8,128)(2,1)S(1)}, u32[]{:S(2)}, u32[]{:S(2)}) collective-permute-start(bf16[2,32,1024]{2,1,0:T(8,128)(2,1)S(1)} %all_gather.9), channel_id=1, source_target_pairs={{0,12},{4,0},{8,4},{12,8},{1,13},{5,1},{9,5},{13,9},{2,14},{6,2},{... | collective-permute-start | bytes 393224 | tf_op jit(solution)/shard_map/ppermute | solution.py:14
  21.7 7.2 %collective-permute-start.1 = (bf16[2,32,1024]{2,1,0:T(8,128)(2,1)S(1)}, bf16[2,32,1024]{2,1,0:T(8,128)(2,1)S(1)}, u32[]{:S(2)}, u32[]{:S(2)}) collective-permute-start(bf16[2,32,1024]{2,1,0:T(8,128)(2,1)S(1)} %collective-permute-done), channel_id=1, source_target_pairs={{0,4},{4,8},{8,12},{12,0},{1,5},{5,9},{9,13},{13,1},{2,6},{6,10},{... | collective-permute-start | bytes 393224 | tf_op jit(solution)/shard_map/ppermute | solution.py:14
  22.6 6.7 %collective-permute-start.4 = (bf16[2,32,1024]{2,1,0:T(8,128)(2,1)S(1)}, bf16[2,32,1024]{2,1,0:T(8,128)(2,1)S(1)}, u32[]{:S(2)}, u32[]{:S(2)}) collective-permute-start(bf16[2,32,1024]{2,1,0:T(8,128)(2,1)S(1)} %collective-permute-done.3), channel_id=1, source_target_pairs={{0,12},{4,0},{8,4},{12,8},{1,13},{5,1},{9,5},{13,9},{2,14},{6,2},{... | collective-permute-start | bytes 393224 | tf_op jit(solution)/shard_map/ppermute | solution.py:14
  28.9 7.9 %collective-permute-start.2 = (bf16[2,32,1024]{2,1,0:T(8,128)(2,1)S(1)}, bf16[2,32,1024]{2,1,0:T(8,128)(2,1)S(1)}, u32[]{:S(2)}, u32[]{:S(2)}) collective-permute-start(bf16[2,32,1024]{2,1,0:T(8,128)(2,1)S(1)} %collective-permute-done.1), channel_id=1, source_target_pairs={{0,4},{4,8},{8,12},{12,0},{1,5},{5,9},{9,13},{13,1},{2,6},{6,10},{... | collective-permute-start | bytes 393224 | tf_op jit(solution)/shard_map/ppermute | solution.py:14
  29.2 8.0 %collective-permute-start.5 = (bf16[2,32,1024]{2,1,0:T(8,128)(2,1)S(1)}, bf16[2,32,1024]{2,1,0:T(8,128)(2,1)S(1)}, u32[]{:S(2)}, u32[]{:S(2)}) collective-permute-start(bf16[2,32,1024]{2,1,0:T(8,128)(2,1)S(1)} %collective-permute-done.4), channel_id=1, source_target_pairs={{0,12},{4,0},{8,4},{12,8},{1,13},{5,1},{9,5},{13,9},{2,14},{6,2},{... | collective-permute-start | bytes 393224 | tf_op jit(solution)/shard_map/ppermute | solution.py:14
  37.3 94.3 %copy-start.4 = (u32[32]{0:T(128)S(1)}, u32[32]{0:T(128)}, u32[]{:S(2)}) copy-start(u32[32]{0:T(128)} %constant.316) | copy-start | bytes 388
  37.3 5.2 %copy-start.1 = (f32[32,1024]{1,0:T(8,128)S(1)}, f32[32,1024]{1,0:T(8,128)}, u32[]{:S(2)}) copy-start(f32[32,1024]{1,0:T(8,128)} %get-tuple-element.783) | copy-start | bytes 393220 | tf_op jit(solution)/shard_map/while
  37.4 5.2 %copy-start.3 = (bf16[1,32,1024]{2,1,0:T(8,128)(2,1)S(1)}, bf16[1,32,1024]{2,1,0:T(8,128)(2,1)}, u32[]{:S(2)}) copy-start(bf16[1,32,1024]{2,1,0:T(8,128)(2,1)} %get-tuple-element.779) | copy-start | bytes 196612 | tf_op jit(solution)/shard_map/while
  47.5 17.6 %copy-start = (f32[1024,1024]{1,0:T(8,128)S(1)}, f32[1024,1024]{1,0:T(8,128)}, u32[]{:S(2)}) copy-start(f32[1024,1024]{1,0:T(8,128)} %get-tuple-element.609) | copy-start | bytes 12582916 | tf_op jit(solution)/shard_map/while/body/eval_jaxpr/cond
  120.3 5.2 %copy-start.1 = (f32[32,1024]{1,0:T(8,128)S(1)}, f32[32,1024]{1,0:T(8,128)}, u32[]{:S(2)}) copy-start(f32[32,1024]{1,0:T(8,128)} %get-tuple-element.783) | copy-start | bytes 393220 | tf_op jit(solution)/shard_map/while
  120.4 5.2 %copy-start.3 = (bf16[1,32,1024]{2,1,0:T(8,128)(2,1)S(1)}, bf16[1,32,1024]{2,1,0:T(8,128)(2,1)}, u32[]{:S(2)}) copy-start(bf16[1,32,1024]{2,1,0:T(8,128)(2,1)} %get-tuple-element.779) | copy-start | bytes 196612 | tf_op jit(solution)/shard_map/while
  125.6 5.2 %copy-start.1 = (f32[32,1024]{1,0:T(8,128)S(1)}, f32[32,1024]{1,0:T(8,128)}, u32[]{:S(2)}) copy-start(f32[32,1024]{1,0:T(8,128)} %get-tuple-element.783) | copy-start | bytes 393220 | tf_op jit(solution)/shard_map/while
  125.6 5.2 %copy-start.3 = (bf16[1,32,1024]{2,1,0:T(8,128)(2,1)S(1)}, bf16[1,32,1024]{2,1,0:T(8,128)(2,1)}, u32[]{:S(2)}) copy-start(bf16[1,32,1024]{2,1,0:T(8,128)(2,1)} %get-tuple-element.779) | copy-start | bytes 196612 | tf_op jit(solution)/shard_map/while
  130.9 0.7 copy-start.2
Sparse Core Ops, SparseCore 0:
  131.7 19.1 all-reduce.2
